TPU v7x, 32 devices: a whole 2x2x4 slice. The times are simulated.
32 devices in a mesh: bx: 4 (over y, x), by: 8 (over z, core).
Axes of the slice: x: 2, y: 2, z: 4, core: 2. Of those that a mesh axis runs over, the one named last changes fastest.
Arguments:
- forcing: float32 [1216, 1024], P('by', 'bx'), may hold values from -20 to 20
- guess: float32 [1216, 1024], P('by', 'bx'), may hold values from -3 to 3
- shift: float32 [1216, 1024], P('by', 'bx'), may hold values from 0.05 to 2
- ocean_mask: int32 [1216, 1024], P('by', 'bx'), may hold values 0 or 1
Outputs:
- solution_field: float32 [1216, 1024], P('by', 'bx')
- residual: float32 [1216, 1024], P('by', 'bx')
- residual_norm: float32 [], replicated
All inputs are finite; a program needn't handle non-finite values. No bound on the sum of `ocean_mask` on one device may be relied on, other than what follows from the above.
Results may differ from a plain program's by a relative error of at most 0.00002.
Values sent between devices are 32-bit elements; how exact they have to be, the bound alone decides.
No kernel may reach another device: no remote copies, remote signals or barrier semaphores. Data moves between devices by JAX's collectives and lax.ppermute only.
A program may use at most 64 MiB of HBM per device.

v0:
```python
import jax
import jax.numpy as jnp
from jax import lax
from jax.sharding import PartitionSpec as P

ITERS = 4
LOW_BOUND = 0.05
HIGH_BOUND = 14.5


def padded_2(block, sides, width):
    for axis, dim in sides:
        count = lax.axis_size(axis)
        forward = [(i, i + 1) for i in range(count - 1)]
        forward.append((count - 1, 0))
        backward = [(target, source) for source, target in forward]
        low = lax.ppermute(
            lax.slice_in_dim(block, block.shape[dim] - width, None, axis=dim), axis, forward
        )
        high = lax.ppermute(lax.slice_in_dim(block, 0, width, axis=dim), axis, backward)
        block = jnp.concatenate([low, block, high], axis=dim)
    return block


def stencil_padded(padded, shift, mask_f):
    center = padded[1:-1, 1:-1]
    sides = padded[2:, 1:-1] + padded[:-2, 1:-1] + padded[1:-1, 2:] + padded[1:-1, :-2]
    corners = padded[2:, 2:] + padded[2:, :-2] + padded[:-2, 2:] + padded[:-2, :-2]
    return mask_f * ((6.0 + shift) * center - sides - 0.5 * corners)


def crop_cycle(values, cycle):
    return values[cycle : values.shape[0] - cycle, cycle : values.shape[1] - cycle]


def local_stencil(values, shift_full, mask_full):
    cycle = (shift_full.shape[0] - values.shape[0]) // 2 + 1
    return stencil_padded(values, crop_cycle(shift_full, cycle), crop_cycle(mask_full, cycle))


def deep_inputs(forcing, guess, shift, mask_f):
    rows, cols = forcing.shape
    depth = ITERS + 1
    stacked = jnp.stack([forcing, guess, shift, mask_f])
    padded = padded_2(stacked, (("bx", 2), ("by", 1)), depth)
    top_rows = stacked[:, rows - depth :, :]
    whole_top = lax.all_gather(top_rows, "bx", axis=2, tiled=True)
    flipped = whole_top[:, ::-1, ::-1]
    extended = jnp.concatenate([flipped[:, :, -depth:], flipped, flipped[:, :, :depth]], axis=2)
    ghost = lax.dynamic_slice_in_dim(extended, lax.axis_index("bx") * cols, cols + 2 * depth, 2)
    row_index = lax.axis_index("by")
    upper_rows = jnp.where(row_index == lax.axis_size("by") - 1, ghost, padded[:, rows + depth :])
    lower_rows = jnp.where(row_index == 0, jnp.zeros_like(ghost), padded[:, :depth])
    return jnp.concatenate([lower_rows, padded[:, depth : rows + depth], upper_rows], axis=1)


def pair_add(first, second):
    total = first[0] + second[0]
    backed = total - first[0]
    error = first[0] - (total - backed) + (second[0] - backed)
    error = error + first[1] + second[1]
    upper = total + error
    lower = error - (upper - total)
    return (upper, lower)


def tree_total(uppers, lowers):
    while uppers.shape[0] > 1:
        if uppers.shape[0] % 2 == 1:
            uppers = jnp.concatenate([uppers, jnp.zeros((1,), uppers.dtype)])
            lowers = jnp.concatenate([lowers, jnp.zeros((1,), lowers.dtype)])
        uppers, lowers = pair_add((uppers[0::2], lowers[0::2]), (uppers[1::2], lowers[1::2]))
    return (uppers[0], lowers[0])


def per_device(forcing, guess, shift, ocean_mask):
    mask_f = ocean_mask.astype(jnp.float32)
    theta = (HIGH_BOUND + LOW_BOUND) / 2.0
    delta = (HIGH_BOUND - LOW_BOUND) / 2.0
    sigma = theta / delta
    rho = 1.0 / sigma
    full = deep_inputs(forcing, guess, shift, mask_f)
    forcing_full = full[0]
    guess_full = full[1]
    shift_full = full[2]
    mask_full = full[3]
    iterate = mask_full * guess_full
    resid = crop_cycle(mask_full * forcing_full, 1) - local_stencil(iterate, shift_full, mask_full)
    direction = resid / theta
    iterate = crop_cycle(iterate, 1)
    for sweep in range(ITERS):
        iterate = iterate + direction
        image = local_stencil(direction, shift_full, mask_full)
        resid = crop_cycle(resid, 1) - image
        rho_next = 1.0 / (2.0 * sigma - rho)
        direction = rho_next * rho * crop_cycle(direction, 1) + 2.0 * rho_next / delta * resid
        rho = rho_next
        iterate = crop_cycle(iterate, 1)
    row_sums = jnp.sum(resid * resid, axis=1)
    upper, lower = tree_total(row_sums, jnp.zeros_like(row_sums))
    all_upper, all_lower = (
        lax.all_gather(upper[None], ("bx", "by"), axis=0, tiled=True),
        lax.all_gather(lower[None], ("bx", "by"), axis=0, tiled=True),
    )
    upper, lower = tree_total(all_upper, all_lower)
    grid_cells = resid.shape[0] * lax.axis_size("by") * resid.shape[1] * lax.axis_size("bx")
    norm_value = jnp.sqrt((upper + lower) / grid_cells)
    return (iterate, resid, norm_value)


def solution(mesh):
    in_specs = (P("by", "bx"), P("by", "bx"), P("by", "bx"), P("by", "bx"))
    out_specs = (P("by", "bx"), P("by", "bx"), P())
    return jax.shard_map(
        per_device, mesh=mesh, in_specs=in_specs, out_specs=out_specs, check_vma=False
    )
```

profile of v0, /device:TPU:0, one launch (start us, length us, event | category | flops | bytes accessed | tf_op | source)
XLA Modules:
  0.0 87.8 jit_solution(3005025311582672974)
XLA Ops:
  0.7 1.0 %convert_bitcast_fusion = f32[1,152,256]{2,1,0:T(8,128)S(1)} fusion(s32[152,256]{1,0:T(8,128)} %param.7), kind=kLoop, calls=%fused_computation.81 | loop fusion | flops 38912 | bytes 311296 | tf_op jit(solution)/shard_map/stack | solution.py:44
  1.7 1.0 %pad_maximum_fusion.1 = f32[4,152,256]{2,1,0:T(8,128)S(1)} fusion(f32[1,152,256]{2,1,0:T(8,128)S(1)} %convert_bitcast_fusion, f32[1,152,256]{2,1,0:T(8,128)S(1)} %bitcast.18, f32[1,152,256]{2,1,0:T(8,128)S(1)} %bitcast.22, f32[1,152,256]{2,1,0:T(8,128)} %bitcast.26), kind=kLoop, calls=%fused_computation.1 | loop fusion | flops 466944 | bytes 1245184 | tf_op jit(solution)/shard_map/stack | solution.py:44
  2.7 0.1 fusion.38
  2.8 3.0 %collective-permute-start = (f32[4,152,5]{2,1,0:T(8,128)S(1)}, f32[4,152,5]{2,1,0:T(8,128)S(1)}, u32[]{:S(2)}, u32[]{:S(2)}) collective-permute-start(f32[4,152,5]{2,1,0:T(8,128)S(1)} %get-tuple-element.62), channel_id=1, source_target_pairs={{0,8},{8,16},{16,24},{24,0},{1,9},{9,17},{17,25},{25,1},{2,10},{10... | collective-permute-start | bytes 36488 | tf_op jit(solution)/shard_map/ppermute | solution.py:17
  5.8 1.0 %collective-permute-start.1 = (f32[4,152,5]{2,1,0:T(8,128)S(1)}, f32[4,152,5]{2,1,0:T(8,128)S(1)}, u32[]{:S(2)}, u32[]{:S(2)}) collective-permute-start(f32[4,152,5]{2,1,0:T(8,128)S(1)} %get-tuple-element.63), channel_id=1, source_target_pairs={{8,0},{16,8},{24,16},{0,24},{9,1},{17,9},{25,17},{1,25},{10,2},{18... | collective-permute-start | bytes 36488 | tf_op jit(solution)/shard_map/ppermute | solution.py:20
  6.9 17.0 %all_gather.9 = f32[4,5,1024]{2,1,0:T(8,128)S(1)} all-gather(f32[4,5,256]{2,1,0:T(8,128)S(1)} %pad_maximum_fusion.8), channel_id=1, replica_groups=mesh['bx'=4,'by'=8] {'bx'}, dimensions={2}, use_global_device_ids=true | all-gather | bytes 102400 | tf_op jit(solution)/shard_map/all_gather | solution.py:47
  24.1 0.7 rev.3
  25.1 3.6 %collective-permute-start.3 = (f32[4,5,266]{2,1,0:T(8,128)S(1)}, f32[4,5,266]{2,1,0:T(8,128)S(1)}, u32[]{:S(2)}, u32[]{:S(2)}) collective-permute-start(f32[4,5,266]{2,1,0:T(8,128)S(1)} %get-tuple-element.58), channel_id=1, source_target_pairs={{1,0},{2,1},{3,2},{4,3},{5,4},{6,5},{7,6},{0,7},{9,8},{10,9},{11,1... | collective-permute-start | bytes 63848 | tf_op jit(solution)/shard_map/ppermute | solution.py:20
  28.7 0.6 collective-permute-done.2
  29.3 1.1 %collective-permute-done.3 = f32[4,5,266]{2,1,0:T(8,128)S(1)} collective-permute-done((f32[4,5,266]{2,1,0:T(8,128)S(1)}, f32[4,5,266]{2,1,0:T(8,128)S(1)}, u32[]{:S(2)}, u32[]{:S(2)}) %collective-permute-start.3) | collective-permute-done | bytes 21312 | tf_op jit(solution)/shard_map/ppermute | solution.py:20
  30.5 0.4 pad_maximum_fusion
  31.2 0.7 broadcast_multiply_fusion
  32.0 0.6 multiply_add_fusion.2
  32.8 0.6 multiply_add_fusion.1
  33.4 0.6 multiply_add_fusion
  34.1 1.4 %multiply_reduce_fusion = (f32[152]{0:T(256)S(1)}, f32[152,256]{1,0:T(8,128)}, f32[152,256]{1,0:T(8,128)}) fusion(f32[154,258]{1,0:T(8,128)S(1)} %get-tuple-element.49, f32[162,266]{1,0:T(8,128)S(1)} %get-tuple-element.60, f32[162,266]{1,0:T(8,128)S(1)} %get-tuple-element.59, f32[154,258]{1,0:T(8,128)S(1)} %get-tuple-element.50, ...), kind=kLoop, calls=%fused_computation.80 | loop fusion | flops 739176 | bytes 2802272 | tf_op jit(solution)/shard_map/reduce_sum | solution.py:99
  35.5 0.2 slice.471
  35.6 0.2 slice.470
  36.1 0.1 slice.473
  38.9 0.6 add_dynamic-update-slice_fusion
  39.5 0.8 subtract_dynamic-update-slice_fusion
  40.3 38.8 %all-reduce.2 = (f32[32]{0:T(128)S(1)}, f32[32]{0:T(128)S(1)}) all-reduce(f32[32]{0:T(128)S(1)} %get-tuple-element.72, f32[32]{0:T(128)S(1)} %subtract_dynamic-update-slice_fusion), channel_id=1, replica_groups=mesh['bx'=4,'by'=8] {'bx','by'}, use_global_device_ids=true, to_apply=%add | all-reduce | flops 64 | bytes 512
  80.8 0.6 fusion.41
  84.1 0.6 fusion.40
  (90 shorter events, 5.7 us)
Async XLA Ops:
  0.6 1.0 %copy-start = (f32[152,256]{1,0:T(8,128)S(1)}, f32[152,256]{1,0:T(8,128)}, u32[]{:S(2)}) copy-start(f32[152,256]{1,0:T(8,128)} %param.6) | copy-start | bytes 466948
  0.6 1.1 %copy-start.1 = (f32[152,256]{1,0:T(8,128)S(1)}, f32[152,256]{1,0:T(8,128)}, u32[]{:S(2)}) copy-start(f32[152,256]{1,0:T(8,128)} %param.5) | copy-start | bytes 466948
  2.7 4.2 %copy-start.2 = (f32[152,256]{1,0:T(8,128)S(1)}, f32[152,256]{1,0:T(8,128)}, u32[]{:S(2)}) copy-start(f32[152,256]{1,0:T(8,128)} %param.4) | copy-start | bytes 466948
  2.8 21.0 %collective-permute-start = (f32[4,152,5]{2,1,0:T(8,128)S(1)}, f32[4,152,5]{2,1,0:T(8,128)S(1)}, u32[]{:S(2)}, u32[]{:S(2)}) collective-permute-start(f32[4,152,5]{2,1,0:T(8,128)S(1)} %get-tuple-element.62), channel_id=1, source_target_pairs={{0,8},{8,16},{16,24},{24,0},{1,9},{9,17},{17,25},{25,1},{2,10},{10... | collective-permute-start | bytes 36488 | tf_op jit(solution)/shard_map/ppermute | solution.py:17
  5.8 18.0 %collective-permute-start.1 = (f32[4,152,5]{2,1,0:T(8,128)S(1)}, f32[4,152,5]{2,1,0:T(8,128)S(1)}, u32[]{:S(2)}, u32[]{:S(2)}) collective-permute-start(f32[4,152,5]{2,1,0:T(8,128)S(1)} %get-tuple-element.63), channel_id=1, source_target_pairs={{8,0},{16,8},{24,16},{0,24},{9,1},{17,9},{25,17},{1,25},{10,2},{18... | collective-permute-start | bytes 36488 | tf_op jit(solution)/shard_map/ppermute | solution.py:20
  24.0 5.4 %collective-permute-start.2 = (f32[4,5,266]{2,1,0:T(8,128)S(1)}, f32[4,5,266]{2,1,0:T(8,128)S(1)}, u32[]{:S(2)}, u32[]{:S(2)}) collective-permute-start(f32[4,5,266]{2,1,0:T(8,128)S(1)} %get-tuple-element.57), channel_id=1, source_target_pairs={{0,1},{1,2},{2,3},{3,4},{4,5},{5,6},{6,7},{7,0},{8,9},{9,10},{10,1... | collective-permute-start | bytes 63848 | tf_op jit(solution)/shard_map/ppermute | solution.py:17
  25.1 5.3 %collective-permute-start.3 = (f32[4,5,266]{2,1,0:T(8,128)S(1)}, f32[4,5,266]{2,1,0:T(8,128)S(1)}, u32[]{:S(2)}, u32[]{:S(2)}) collective-permute-start(f32[4,5,266]{2,1,0:T(8,128)S(1)} %get-tuple-element.58), channel_id=1, source_target_pairs={{1,0},{2,1},{3,2},{4,3},{5,4},{6,5},{7,6},{0,7},{9,8},{10,9},{11,1... | collective-permute-start | bytes 63848 | tf_op jit(solution)/shard_map/ppermute | solution.py:20
where the time goes:
time: 88.3 us; the launch traced here: 87.8 us
  blocking collectives  55.8 us (63%)
  other arithmetic  8.6 us (10%)
  starting transfers between devices  7.68 us (9%)
  local copies, waits for them, and re-layouts  7.26 us (8%)
  between operations  6.75 us (8%)
  waiting for transfers between devices  1.75 us (2%)
    unnamed x1, blocking collectives  38.8 us
    all_gather x1, blocking collectives, deep_inputs(): whole_top = lax.all_gather(top_rows, 'bx', axis=2, tiled=True)  17 us
    ppermute x2, starting transfers between devices, padded_2(): lax.ppermute(lax.slice_in_dim(block, 0, width, axis=dim), axis, backward)  4.6 us
    ppermute x2, starting transfers between devices, padded_2(): lax.ppermute(lax.slice_in_dim(block, block.shape[dim] - width, None, axis...  3.07 us
    add x3, other arithmetic, per_device(): rho_next * rho * crop_cycle(direction, 1) + 2.0 * rho_next / delta * resid  1.94 us
    another operation x2, other arithmetic, deep_inputs(): stacked = jnp.stack([forcing, guess, shift, mask_f])  1.93 us
    slice x12, local copies, waits for them, and re-layouts, tree_total(): uppers[1::2]  1.78 us
  transfers between devices with their start and end apart: 4, of which 2 were waited for; matrix products, arithmetic and copies ran while one was open for 1% of the time, Pallas kernels for 0%

commit v1 on v0

--- a/solution.py
+++ b/solution.py
@@ -44,7 +44,7 @@
     stacked = jnp.stack([forcing, guess, shift, mask_f])
     padded = padded_2(stacked, (("bx", 2), ("by", 1)), depth)
     top_rows = stacked[:, rows - depth :, :]
-    whole_top = lax.all_gather(top_rows, "bx", axis=2, tiled=True)
+    whole_top = jnp.concatenate(lax.all_gather(top_rows, "bx"), axis=2)
     flipped = whole_top[:, ::-1, ::-1]
     extended = jnp.concatenate([flipped[:, :, -depth:], flipped, flipped[:, :, :depth]], axis=2)
     ghost = lax.dynamic_slice_in_dim(extended, lax.axis_index("bx") * cols, cols + 2 * depth, 2)

time: 88.3 us -> 92.8 us (1.051)
  local copies, waits for them, and re-layouts: 7.26 us -> 11.3 us
    concatenate x1, other arithmetic: 0.43 us -> 2.33 us  [deep_inputs(): jnp.concatenate([lower_rows, padded[:, depth:rows + depth], upper_rows],...]
    unnamed x8 -> x9, local copies, waits for them, and re-layouts: 0.08 us -> 1.62 us
    another operation x0 -> x4, local copies, waits for them, and re-layouts: none -> 1.38 us  [deep_inputs(): stacked = jnp.stack([forcing, guess, shift, mask_f])]
    another operation x2 -> x1, other arithmetic: 1.93 us -> 0.59 us  [deep_inputs(): stacked = jnp.stack([forcing, guess, shift, mask_f])]
where the time goes in v1:
time: 92.8 us; the launch traced here: 92.4 us
  blocking collectives  55.7 us (60%)
  local copies, waits for them, and re-layouts  11.3 us (12%)
  other arithmetic  9.4 us (10%)
  starting transfers between devices  7.68 us (8%)
  between operations  6.8 us (7%)
  waiting for transfers between devices  1.57 us (2%)
    unnamed x1, blocking collectives  38.8 us
    all_gather x1, blocking collectives, deep_inputs(): whole_top = jnp.concatenate(lax.all_gather(top_rows, 'bx'), axis=2)  16.9 us
    ppermute x2, starting transfers between devices, padded_2(): lax.ppermute(lax.slice_in_dim(block, 0, width, axis=dim), axis, backward)  4.6 us
    ppermute x2, starting transfers between devices, padded_2(): lax.ppermute(lax.slice_in_dim(block, block.shape[dim] - width, None, axis...  3.07 us
    concatenate x1, other arithmetic, deep_inputs(): jnp.concatenate([lower_rows, padded[:, depth:rows + depth], upper_rows],...  2.33 us
    add x3, other arithmetic, per_device(): rho_next * rho * crop_cycle(direction, 1) + 2.0 * rho_next / delta * resid  1.94 us
  transfers between devices with their start and end apart: 4, of which 2 were waited for; matrix products, arithmetic and copies ran while one was open for 1% of the time, Pallas kernels for 0%

profile of v1, /device:TPU:0, one launch (start us, length us, event | category | flops | bytes accessed | tf_op | source)
XLA Modules:
  0.0 92.4 jit_solution(6286985885734415384)
XLA Ops:
  0.6 1.1 %stack.15 = f32[1,152,256]{2,0,1:T(1,128)S(1)} reshape(f32[152,256]{1,0:T(8,128)} %param.4) | data formatting | bytes 311296 | tf_op jit(solution)/shard_map/stack | solution.py:44
  1.8 0.8 copy-done.1
  2.7 0.8 copy-done.2
  3.7 0.6 pad_maximum_fusion.1
  4.3 0.2 fusion.39
  4.5 3.0 %collective-permute-start = (f32[4,152,5]{2,0,1:T(4,128)S(1)}, f32[4,152,5]{2,0,1:T(4,128)S(1)}, u32[]{:S(2)}, u32[]{:S(2)}) collective-permute-start(f32[4,152,5]{2,0,1:T(4,128)S(1)} %get-tuple-element.63), channel_id=1, source_target_pairs={{0,8},{8,16},{16,24},{24,0},{1,9},{9,17},{17,25},{25,1},{2,10},{10... | collective-permute-start | bytes 36488 | tf_op jit(solution)/shard_map/ppermute | solution.py:17
  7.5 1.0 %collective-permute-start.1 = (f32[4,152,5]{2,0,1:T(4,128)S(1)}, f32[4,152,5]{2,0,1:T(4,128)S(1)}, u32[]{:S(2)}, u32[]{:S(2)}) collective-permute-start(f32[4,152,5]{2,0,1:T(4,128)S(1)} %get-tuple-element.64), channel_id=1, source_target_pairs={{8,0},{16,8},{24,16},{0,24},{9,1},{17,9},{25,17},{1,25},{10,2},{18... | collective-permute-start | bytes 36488 | tf_op jit(solution)/shard_map/ppermute | solution.py:20
  8.6 16.9 %all-gather = f32[16,5,256]{2,1,0:T(8,128)S(1)} all-gather(f32[4,5,256]{2,1,0:T(8,128)S(1)} %copy.12), channel_id=2, replica_groups=mesh['bx'=4,'by'=8] {'bx'}, dimensions={0}, use_global_device_ids=true | all-gather | bytes 102400 | tf_op jit(solution)/shard_map/all_gather | solution.py:47
  26.0 0.8 rev.3
  27.2 3.6 %collective-permute-start.3 = (f32[4,5,266]{2,0,1:T(4,128)S(1)}, f32[4,5,266]{2,0,1:T(4,128)S(1)}, u32[]{:S(2)}, u32[]{:S(2)}) collective-permute-start(f32[4,5,266]{2,0,1:T(4,128)S(1)} %get-tuple-element.58), channel_id=1, source_target_pairs={{1,0},{2,1},{3,2},{4,3},{5,4},{6,5},{7,6},{0,7},{9,8},{10,9},{11,1... | collective-permute-start | bytes 63848 | tf_op jit(solution)/shard_map/ppermute | solution.py:20
  30.8 0.3 collective-permute-done.2
  31.1 1.3 %collective-permute-done.3 = f32[4,5,266]{2,0,1:T(4,128)S(1)} collective-permute-done((f32[4,5,266]{2,0,1:T(4,128)S(1)}, f32[4,5,266]{2,0,1:T(4,128)S(1)}, u32[]{:S(2)}, u32[]{:S(2)}) %collective-permute-start.3) | collective-permute-done | bytes 21312 | tf_op jit(solution)/shard_map/ppermute | solution.py:20
  32.4 2.3 %pad_maximum_fusion = f32[4,162,266]{2,0,1:T(4,128)S(1)} fusion(f32[4,5,266]{2,0,1:T(4,128)S(1)} %dynamic-slice_select_fusion, f32[4,152,5]{2,0,1:T(4,128)S(1)} %collective-permute-done.1, f32[1,152,256]{2,0,1:T(1,128)S(1)} %stack.18, f32[1,152,256]{2,0,1:T(1,128)S(1)} %stack.17, f32[1,152,256]{2,0,1:T(1,128)S(1)} %stack.16, f32[1,152,256]{2,0,1:T(1,128)S(1)} %stack.15, ...), kind=kLoop, calls=%fused_computation | loop fusion | flops 1206576 | bytes 1378944 | tf_op jit(solution)/shard_map/concatenate | solution.py:54
  34.8 0.7 fusion.38
  35.7 0.7 broadcast_multiply_fusion
  36.5 0.6 multiply_add_fusion.2
  37.3 0.6 multiply_add_fusion.1
  38.0 0.6 multiply_add_fusion
  38.6 1.4 %multiply_reduce_fusion = (f32[152]{0:T(256)S(1)}, f32[152,256]{1,0:T(8,128)}, f32[152,256]{1,0:T(8,128)}) fusion(f32[154,258]{1,0:T(8,128)S(1)} %get-tuple-element.49, f32[162,266]{1,0:T(8,128)S(1)} %bitcast.24, f32[162,266]{1,0:T(8,128)S(1)} %get-tuple-element.76, f32[154,258]{1,0:T(8,128)S(1)} %get-tuple-element.50, f32[154,258]{1,0:T(8,128)S(1)} %get-tuple-element.66, ...), kind=kLoop, calls=%fused_computation.80 | loop fusion | flops 739176 | bytes 2802272 | tf_op jit(solution)/shard_map/reduce_sum | solution.py:99
  43.5 0.6 add_dynamic-update-slice_fusion
  44.1 0.8 subtract_dynamic-update-slice_fusion
  45.0 38.8 %all-reduce.2 = (f32[32]{0:T(128)S(1)}, f32[32]{0:T(128)S(1)}) all-reduce(f32[32]{0:T(128)S(1)} %get-tuple-element.73, f32[32]{0:T(128)S(1)} %subtract_dynamic-update-slice_fusion), channel_id=1, replica_groups=mesh['bx'=4,'by'=8] {'bx','by'}, use_global_device_ids=true, to_apply=%add | all-reduce | flops 64 | bytes 512
  85.4 0.6 fusion.42
  88.7 0.6 fusion.41
  (100 shorter events, 6.9 us)
Async XLA Ops:
  0.6 1.1 %copy-start = (f32[152,256]{1,0:T(8,128)S(1)}, f32[152,256]{1,0:T(8,128)}, u32[]{:S(2)}) copy-start(f32[152,256]{1,0:T(8,128)} %param.5) | copy-start | bytes 466948
  1.7 0.9 copy-start.1
  2.6 0.9 copy-start.2
  4.5 21.2 %collective-permute-start = (f32[4,152,5]{2,0,1:T(4,128)S(1)}, f32[4,152,5]{2,0,1:T(4,128)S(1)}, u32[]{:S(2)}, u32[]{:S(2)}) collective-permute-start(f32[4,152,5]{2,0,1:T(4,128)S(1)} %get-tuple-element.63), channel_id=1, source_target_pairs={{0,8},{8,16},{16,24},{24,0},{1,9},{9,17},{17,25},{25,1},{2,10},{10... | collective-permute-start | bytes 36488 | tf_op jit(solution)/shard_map/ppermute | solution.py:17
  7.5 18.2 %collective-permute-start.1 = (f32[4,152,5]{2,0,1:T(4,128)S(1)}, f32[4,152,5]{2,0,1:T(4,128)S(1)}, u32[]{:S(2)}, u32[]{:S(2)}) collective-permute-start(f32[4,152,5]{2,0,1:T(4,128)S(1)} %get-tuple-element.64), channel_id=1, source_target_pairs={{8,0},{16,8},{24,16},{0,24},{9,1},{17,9},{25,17},{1,25},{10,2},{18... | collective-permute-start | bytes 36488 | tf_op jit(solution)/shard_map/ppermute | solution.py:20
  25.9 5.2 %collective-permute-start.2 = (f32[4,5,266]{2,0,1:T(4,128)S(1)}, f32[4,5,266]{2,0,1:T(4,128)S(1)}, u32[]{:S(2)}, u32[]{:S(2)}) collective-permute-start(f32[4,5,266]{2,0,1:T(4,128)S(1)} %get-tuple-element.57), channel_id=1, source_target_pairs={{0,1},{1,2},{2,3},{3,4},{4,5},{5,6},{6,7},{7,0},{8,9},{9,10},{10,1... | collective-permute-start | bytes 63848 | tf_op jit(solution)/shard_map/ppermute | solution.py:17
  27.2 5.2 %collective-permute-start.3 = (f32[4,5,266]{2,0,1:T(4,128)S(1)}, f32[4,5,266]{2,0,1:T(4,128)S(1)}, u32[]{:S(2)}, u32[]{:S(2)}) collective-permute-start(f32[4,5,266]{2,0,1:T(4,128)S(1)} %get-tuple-element.58), channel_id=1, source_target_pairs={{1,0},{2,1},{3,2},{4,3},{5,4},{6,5},{7,6},{0,7},{9,8},{10,9},{11,1... | collective-permute-start | bytes 63848 | tf_op jit(solution)/shard_map/ppermute | solution.py:20
